TPU v7x, 32 devices: a whole 2x2x4 slice. The times are simulated.
32 devices in a mesh: seq: 4 (over z), ctx: 8 (over y, x, core).
Axes of the slice: x: 2, y: 2, z: 4, core: 2. Of those that a mesh axis runs over, the one named last changes fastest.
Arguments:
- hidden_states: bfloat16 [4, 1024, 1024], P('seq', 'ctx'), may hold values from -6 to 6
- positions: int32 [4, 1024], P('seq'), may hold values from 0 to 1023, as said below
- gain_first: bfloat16 [1024], P(('seq', 'ctx')), may hold values from 0.25 to 1.75
- weight_query: bfloat16 [1024, 2048], P(('seq', 'ctx')), may hold values from -0.1875 to 0.1875
- key_weight_matrix: bfloat16 [1024, 1024], P(('seq', 'ctx')), may hold values from -0.1875 to 0.1875
- value_weight_matrix: bfloat16 [1024, 1024], P(('seq', 'ctx')), may hold values from -0.1875 to 0.1875
- gain_query: bfloat16 [128], P(('seq', 'ctx')), may hold values from 0.25 to 1.75
- gain_key: bfloat16 [128], P(('seq', 'ctx')), may hold values from 0.25 to 1.75
- weight_output: bfloat16 [2048, 1024], P(('seq', 'ctx')), may hold values from -2 to 2
- gain_second: bfloat16 [1024], P(('seq', 'ctx')), may hold values from 0.25 to 1.75
- weight_gate: bfloat16 [1024, 3072], P(('seq', 'ctx')), may hold values from -0.1875 to 0.1875
- weight_up: bfloat16 [1024, 3072], P(('seq', 'ctx')), may hold values from -0.1875 to 0.1875
- weight_down: bfloat16 [3072, 1024], P(('seq', 'ctx')), may hold values from -0.109375 to 0.109375
- output_cotangent: bfloat16 [4, 1024, 1024], P('seq', 'ctx'), may hold values from -6 to 6
Outputs:
- layer_output: bfloat16 [4, 1024, 1024], P('seq', 'ctx')
- hidden_gradient: float32 [4, 1024, 1024], P('seq', 'ctx')
- change_first: float32 [1024], P(('seq', 'ctx'))
- delta_query: float32 [1024, 2048], P(('seq', 'ctx'))
- delta_key: float32 [1024, 1024], P(('seq', 'ctx'))
- delta_value: float32 [1024, 1024], P(('seq', 'ctx'))
- change_query: float32 [128], P(('seq', 'ctx'))
- change_key: float32 [128], P(('seq', 'ctx'))
- delta_output: float32 [2048, 1024], P(('seq', 'ctx'))
- change_second: float32 [1024], P(('seq', 'ctx'))
- delta_gate: float32 [1024, 3072], P(('seq', 'ctx'))
- delta_up: float32 [1024, 3072], P(('seq', 'ctx'))
- delta_down: float32 [3072, 1024], P(('seq', 'ctx'))
Inputs may be any that keep to these rules, and one draw needn't show every extreme that they name: In every sequence each position 0 to 1023 occurs once; the 128 stored tokens of one device of ctx are two runs of 64 consecutive ascending positions, each run starting at a multiple of 64, and their two run numbers sum to 15.
All inputs are finite; a program needn't handle non-finite values.
Results may differ from a plain program's by a relative error of at most 0.023.
Values may be sent and summed in bfloat16 or wider, within the bound.
A program may use at most 104 MiB of HBM per device.

v0:
```python
import jax
import jax.numpy as jnp
from jax import lax
from jax.sharding import PartitionSpec as P

QUERY_HEAD_COUNT = 16
KEY_VALUE_HEADS = 8
HEAD_DIMENSION = 128
EPS = 1e-06
THETA = 1000000.0
NEGATIVE = -1e30


def inverse_root(values):
    return lax.rsqrt(jnp.mean(values * values, axis=-1, keepdims=True) + EPS)


def angles(places, head_size):
    half_size = head_size // 2
    frequency = jnp.power(THETA, -jnp.arange(half_size, dtype=jnp.float32) * (2.0 / head_size))
    phases = places.astype(jnp.float32)[:, None] * frequency[None, :]
    phases = jnp.concatenate([phases, phases], axis=-1)
    return (jnp.cos(phases), jnp.sin(phases))


def rotate(values, cosines, sines):
    half_size = values.shape[-1] // 2
    turned = jnp.concatenate([-values[..., half_size:], values[..., :half_size]], axis=-1)
    return values * cosines + turned * sines


def rotate_back(upstream, cosines, sines):
    half_size = upstream.shape[-1] // 2
    scaled = upstream * sines
    turned = jnp.concatenate([scaled[..., half_size:], -scaled[..., :half_size]], axis=-1)
    return upstream * cosines + turned


def norm_backward(normed_grad, normed, inverse):
    return inverse * (normed_grad - normed * jnp.mean(normed_grad * normed, axis=-1, keepdims=True))


def local(
    hidden_states,
    positions,
    gain_first,
    weight_query,
    key_weight_matrix,
    value_weight_matrix,
    gain_query,
    gain_key,
    weight_output,
    gain_second,
    weight_gate,
    weight_up,
    weight_down,
    output_cotangent,
):
    tokens = hidden_states.shape[1]
    sequence_length = positions.shape[1]
    head_size = HEAD_DIMENSION
    query_heads = QUERY_HEAD_COUNT
    key_head_rows = KEY_VALUE_HEADS
    group_width = query_heads // key_head_rows
    scale_factor = head_size ** (-0.5)
    key_places = positions[0]
    own_places = lax.dynamic_slice_in_dim(key_places, lax.axis_index("ctx") * tokens, tokens)
    causal_mask = key_places[None, :] <= own_places[:, None]
    cosines, sines = angles(own_places, head_size)
    cosine_heads = cosines[:, None, :]
    sine_heads = sines[:, None, :]
    residual = hidden_states[0].astype(jnp.float32)
    first_gains, query_full, key_full, value_full, query_gains, key_gains, output_full = (
        lax.all_gather(gain_first, ("seq", "ctx"), axis=0, tiled=True),
        lax.all_gather(weight_query, ("seq", "ctx"), axis=0, tiled=True),
        lax.all_gather(key_weight_matrix, ("seq", "ctx"), axis=0, tiled=True),
        lax.all_gather(value_weight_matrix, ("seq", "ctx"), axis=0, tiled=True),
        lax.all_gather(gain_query, ("seq", "ctx"), axis=0, tiled=True),
        lax.all_gather(gain_key, ("seq", "ctx"), axis=0, tiled=True),
        lax.all_gather(weight_output, ("seq", "ctx"), axis=0, tiled=True),
    )
    first_scale = first_gains.astype(jnp.float32)
    query_scale = query_gains.astype(jnp.float32)
    key_scale = key_gains.astype(jnp.float32)
    first_inverse = inverse_root(residual)
    first_normed = residual * first_inverse
    leading_input = (first_normed * first_scale).astype(jnp.bfloat16)
    query_linear = jnp.dot(leading_input, query_full, preferred_element_type=jnp.float32).reshape(
        tokens, query_heads, head_size
    )
    key_projected = jnp.dot(leading_input, key_full, preferred_element_type=jnp.float32).reshape(
        tokens, key_head_rows, head_size
    )
    value_local = jnp.dot(leading_input, value_full, preferred_element_type=jnp.float32).astype(
        jnp.bfloat16
    )
    query_inverse = inverse_root(query_linear)
    query_normed = query_linear * query_inverse
    key_inverse = inverse_root(key_projected)
    key_normed = key_projected * key_inverse
    rotary_query = rotate(query_normed * query_scale, cosine_heads, sine_heads).astype(jnp.bfloat16)
    key_rotated = rotate(key_normed * key_scale, cosine_heads, sine_heads).astype(jnp.bfloat16)
    keys_all, values_all = (
        lax.all_gather(
            key_rotated.reshape(tokens, key_head_rows * head_size), "ctx", axis=0, tiled=True
        ),
        lax.all_gather(value_local, "ctx", axis=0, tiled=True),
    )
    query_blocks = rotary_query.reshape(tokens, key_head_rows, group_width, head_size)
    key_blocks = keys_all.reshape(sequence_length, key_head_rows, head_size)
    value_blocks = values_all.reshape(sequence_length, key_head_rows, head_size)

    def head_scores(head_index):
        query_head = lax.dynamic_index_in_dim(query_blocks, head_index, 1, keepdims=False)
        key_head = lax.dynamic_index_in_dim(key_blocks, head_index, 1, keepdims=False)
        value_head = lax.dynamic_index_in_dim(value_blocks, head_index, 1, keepdims=False)
        raw_scores = (
            jnp.einsum("qgd,kd->gqk", query_head, key_head, preferred_element_type=jnp.float32)
            * scale_factor
        )
        return (
            query_head,
            key_head,
            value_head,
            jnp.where(causal_mask[None], raw_scores, NEGATIVE),
        )

    def forward_head(head_index, carry):
        outputs, log_sums = carry
        query_head, key_head, value_head, scores = head_scores(head_index)
        row_max = jnp.max(scores, axis=-1, keepdims=True)
        exponent = jnp.exp(scores - row_max)
        row_total = jnp.sum(exponent, axis=-1, keepdims=True)
        weights_low = (exponent / row_total).astype(jnp.bfloat16)
        head_output = jnp.einsum(
            "gqk,kd->qgd", weights_low, value_head, preferred_element_type=jnp.float32
        )
        log_total = row_max[..., 0] + jnp.log(row_total[..., 0])
        return (
            lax.dynamic_update_index_in_dim(outputs, head_output, head_index, 1),
            lax.dynamic_update_index_in_dim(log_sums, log_total, head_index, 0),
        )

    start_carry = (
        jnp.zeros((tokens, key_head_rows, group_width, head_size), jnp.float32),
        jnp.zeros((key_head_rows, group_width, tokens), jnp.float32),
    )
    attention, log_totals = lax.fori_loop(0, key_head_rows, forward_head, start_carry)
    attention_low = attention.reshape(tokens, query_heads * head_size).astype(jnp.bfloat16)
    middle = residual + jnp.dot(attention_low, output_full, preferred_element_type=jnp.float32)
    second_gains, gate_full, up_full, down_full = (
        lax.all_gather(gain_second, ("seq", "ctx"), axis=0, tiled=True),
        lax.all_gather(weight_gate, ("seq", "ctx"), axis=0, tiled=True),
        lax.all_gather(weight_up, ("seq", "ctx"), axis=0, tiled=True),
        lax.all_gather(weight_down, ("seq", "ctx"), axis=0, tiled=True),
    )
    second_scale = second_gains.astype(jnp.float32)
    second_inverse = inverse_root(middle)
    second_normed = middle * second_inverse
    second_input = (second_normed * second_scale).astype(jnp.bfloat16)
    gate_linear = jnp.dot(second_input, gate_full, preferred_element_type=jnp.float32)
    up_linear = jnp.dot(second_input, up_full, preferred_element_type=jnp.float32)
    sigmoid_gate = jax.nn.sigmoid(gate_linear)
    silu_gate = gate_linear * sigmoid_gate
    activation = (silu_gate * up_linear).astype(jnp.bfloat16)
    layer_output = (
        middle + jnp.dot(activation, down_full, preferred_element_type=jnp.float32)
    ).astype(jnp.bfloat16)
    gate_back, up_back, down_back = (
        lax.all_gather(weight_gate, ("seq", "ctx"), axis=0, tiled=True),
        lax.all_gather(weight_up, ("seq", "ctx"), axis=0, tiled=True),
        lax.all_gather(weight_down, ("seq", "ctx"), axis=0, tiled=True),
    )
    upstream = output_cotangent[0].astype(jnp.float32)
    upstream_low = upstream.astype(jnp.bfloat16)
    delta_down = lax.psum_scatter(
        jnp.dot(activation.T, upstream_low, preferred_element_type=jnp.float32),
        ("seq", "ctx"),
        scatter_dimension=0,
        tiled=True,
    )
    act_grad = jnp.dot(upstream_low, down_back.T, preferred_element_type=jnp.float32)
    gate_low = (
        act_grad * up_linear * sigmoid_gate * (1.0 + gate_linear * (1.0 - sigmoid_gate))
    ).astype(jnp.bfloat16)
    up_low = (act_grad * silu_gate).astype(jnp.bfloat16)
    second_input_grad = jnp.dot(
        gate_low, gate_back.T, preferred_element_type=jnp.float32
    ) + jnp.dot(up_low, up_back.T, preferred_element_type=jnp.float32)
    second_gain_term = jnp.sum(second_input_grad * second_normed, axis=0)
    middle_grad = upstream + norm_backward(
        second_input_grad * second_scale, second_normed, second_inverse
    )
    hidden_units = gate_low.shape[1]
    both_low = jnp.concatenate([gate_low, up_low], axis=1)
    both_delta = lax.psum_scatter(
        jnp.dot(second_input.T, both_low, preferred_element_type=jnp.float32),
        ("seq", "ctx"),
        scatter_dimension=0,
        tiled=True,
    )
    delta_gate = both_delta[:, :hidden_units]
    delta_up = both_delta[:, hidden_units:]
    query_back, key_back, value_back, output_back = (
        lax.all_gather(weight_query, ("seq", "ctx"), axis=0, tiled=True),
        lax.all_gather(key_weight_matrix, ("seq", "ctx"), axis=0, tiled=True),
        lax.all_gather(value_weight_matrix, ("seq", "ctx"), axis=0, tiled=True),
        lax.all_gather(weight_output, ("seq", "ctx"), axis=0, tiled=True),
    )
    middle_low = middle_grad.astype(jnp.bfloat16)
    delta_output = lax.psum_scatter(
        jnp.dot(attention_low.T, middle_low, preferred_element_type=jnp.float32),
        ("seq", "ctx"),
        scatter_dimension=0,
        tiled=True,
    )
    attention_grad = jnp.dot(middle_low, output_back.T, preferred_element_type=jnp.float32).astype(
        jnp.bfloat16
    )
    attention_grad = attention_grad.reshape(tokens, key_head_rows, group_width, head_size)

    def backward_head(head_index, carry):
        query_sums, key_sums, value_sums = carry
        query_head, key_head, value_head, scores = head_scores(head_index)
        upstream_head = lax.dynamic_index_in_dim(attention_grad, head_index, 1, keepdims=False)
        log_head = lax.dynamic_index_in_dim(log_totals, head_index, 0, keepdims=False)
        probabilities = jnp.exp(scores - log_head[..., None])
        probabilities_low = probabilities.astype(jnp.bfloat16)
        prob_grad = jnp.einsum(
            "qgd,kd->gqk", upstream_head, value_head, preferred_element_type=jnp.float32
        )
        row_inner = jnp.sum(probabilities * prob_grad, axis=-1, keepdims=True)
        score_grad = (probabilities * (prob_grad - row_inner) * scale_factor).astype(jnp.bfloat16)
        query_part = jnp.einsum(
            "gqk,kd->qgd", score_grad, key_head, preferred_element_type=jnp.float32
        )
        key_part = jnp.einsum(
            "gqk,qgd->kd", score_grad, query_head, preferred_element_type=jnp.float32
        )
        value_part = jnp.einsum(
            "gqk,qgd->kd", probabilities_low, upstream_head, preferred_element_type=jnp.float32
        )
        return (
            lax.dynamic_update_index_in_dim(query_sums, query_part, head_index, 1),
            lax.dynamic_update_index_in_dim(key_sums, key_part, head_index, 1),
            lax.dynamic_update_index_in_dim(value_sums, value_part, head_index, 1),
        )

    back_carry = (
        jnp.zeros((tokens, key_head_rows, group_width, head_size), jnp.float32),
        jnp.zeros((sequence_length, key_head_rows, head_size), jnp.float32),
        jnp.zeros((sequence_length, key_head_rows, head_size), jnp.float32),
    )
    query_sums, key_sums, value_sums = lax.fori_loop(0, key_head_rows, backward_head, back_carry)
    key_total, value_total = (
        lax.psum_scatter(
            key_sums.reshape(sequence_length, key_head_rows * head_size).astype(jnp.bfloat16),
            "ctx",
            scatter_dimension=0,
            tiled=True,
        ).astype(jnp.float32),
        lax.psum_scatter(
            value_sums.reshape(sequence_length, key_head_rows * head_size).astype(jnp.bfloat16),
            "ctx",
            scatter_dimension=0,
            tiled=True,
        ).astype(jnp.float32),
    )
    value_grad_low = value_total.astype(jnp.bfloat16)
    key_pre = rotate_back(
        key_total.reshape(tokens, key_head_rows, head_size), cosine_heads, sine_heads
    )
    key_gain_term = jnp.sum(key_pre * key_normed, axis=(0, 1))
    key_low = norm_backward(key_pre * key_scale, key_normed, key_inverse).astype(jnp.bfloat16)
    key_low = key_low.reshape(tokens, key_head_rows * head_size)
    query_pre = rotate_back(
        query_sums.reshape(tokens, query_heads, head_size), cosine_heads, sine_heads
    )
    query_gain_term = jnp.sum(query_pre * query_normed, axis=(0, 1))
    query_low = norm_backward(query_pre * query_scale, query_normed, query_inverse).astype(
        jnp.bfloat16
    )
    query_low = query_low.reshape(tokens, query_heads * head_size)
    first_input_grad = (
        jnp.dot(query_low, query_back.T, preferred_element_type=jnp.float32)
        + jnp.dot(key_low, key_back.T, preferred_element_type=jnp.float32)
        + jnp.dot(value_grad_low, value_back.T, preferred_element_type=jnp.float32)
    )
    first_gain_term = jnp.sum(first_input_grad * first_normed, axis=0)
    hidden_gradient = middle_grad + norm_backward(
        first_input_grad * first_scale, first_normed, first_inverse
    )
    query_term = jnp.dot(leading_input.T, query_low, preferred_element_type=jnp.float32)
    key_term = jnp.dot(leading_input.T, key_low, preferred_element_type=jnp.float32)
    value_term = jnp.dot(leading_input.T, value_grad_low, preferred_element_type=jnp.float32)
    change_first, delta_query, delta_key, delta_value, change_query, change_key, change_second = (
        lax.psum_scatter(first_gain_term, ("seq", "ctx"), scatter_dimension=0, tiled=True),
        lax.psum_scatter(query_term, ("seq", "ctx"), scatter_dimension=0, tiled=True),
        lax.psum_scatter(key_term, ("seq", "ctx"), scatter_dimension=0, tiled=True),
        lax.psum_scatter(value_term, ("seq", "ctx"), scatter_dimension=0, tiled=True),
        lax.psum_scatter(query_gain_term, ("seq", "ctx"), scatter_dimension=0, tiled=True),
        lax.psum_scatter(key_gain_term, ("seq", "ctx"), scatter_dimension=0, tiled=True),
        lax.psum_scatter(second_gain_term, ("seq", "ctx"), scatter_dimension=0, tiled=True),
    )
    return (
        layer_output[None],
        hidden_gradient[None],
        change_first,
        delta_query,
        delta_key,
        delta_value,
        change_query,
        change_key,
        delta_output,
        change_second,
        delta_gate,
        delta_up,
        delta_down,
    )


def solution(mesh):
    return jax.shard_map(
        local,
        mesh=mesh,
        in_specs=(
            P("seq", "ctx", None),
            P("seq", None),
            P(("seq", "ctx")),
            P(("seq", "ctx"), None),
            P(("seq", "ctx"), None),
            P(("seq", "ctx"), None),
            P(("seq", "ctx")),
            P(("seq", "ctx")),
            P(("seq", "ctx"), None),
            P(("seq", "ctx")),
            P(("seq", "ctx"), None),
            P(("seq", "ctx"), None),
            P(("seq", "ctx"), None),
            P("seq", "ctx", None),
        ),
        out_specs=(
            P("seq", "ctx", None),
            P("seq", "ctx", None),
            P(("seq", "ctx")),
            P(("seq", "ctx"), None),
            P(("seq", "ctx"), None),
            P(("seq", "ctx"), None),
            P(("seq", "ctx")),
            P(("seq", "ctx")),
            P(("seq", "ctx"), None),
            P(("seq", "ctx")),
            P(("seq", "ctx"), None),
            P(("seq", "ctx"), None),
            P(("seq", "ctx"), None),
        ),
        check_vma=False,
    )
```

profile of v0, /device:TPU:0, one launch (start us, length us, event | category | flops | bytes accessed | tf_op | source)
XLA Modules:
  0.0 1713.3 jit_solution(6148967494213294258)
XLA Ops:
  12.1 42.2 %all-reduce.9 = (bf16[1024]{0:T(1024)(128)(2,1)S(1)}, bf16[128]{0:T(256)(128)(2,1)S(1)}, bf16[128]{0:T(256)(128)(2,1)S(1)}, bf16[1024]{0:T(1024)(128)(2,1)S(1)}) all-reduce(bf16[1024]{0:T(1024)(128)(2,1)S(1)} %dynamic-update-slice, bf16[128]{0:T(256)(128)(2,1)S(1)} %dynamic-update-slice.1, ...), channel_id=1, replica_groups=mesh['seq'=4,'ctx'=8] {'seq','ctx'}, use_global_device_ids=true, to_apply=%add | all-reduce | flops 2304 | bytes 9216
  55.5 14.4 all-gather.10.cloned.1.call-done
  69.9 2.9 convolution_convert_fusion.1
  73.8 54.1 %all-gather.14.cloned.1.call-done = bf16[1024,1024]{1,0:T(8,128)(2,1)} async-done(((bf16[32,1024]{1,0:T(8,128)(2,1)}), bf16[1024,1024]{1,0:T(8,128)(2,1)}) %all-gather.14.cloned.1.call-update) | async-done | bytes 2097168 | tf_op jit(solution)/shard_map/all_gather | solution.py:76
  127.8 2.9 copy.54
  137.5 19.5 %all-gather.12.cloned.1.call-done = bf16[1024,1024]{1,0:T(8,128)(2,1)} async-done(((bf16[128,1024]{1,0:T(8,128)(2,1)}), bf16[1024,1024]{1,0:T(8,128)(2,1)}) %all-gather.12.cloned.1.call-update) | async-done | bytes 2097168 | tf_op jit(solution)/shard_map/all_gather | solution.py:107
  157.0 3.4 copy_bitcast_fusion.3
  161.0 3.0 copy.56
  164.0 23.4 %all-gather.16.cloned.1.call-done = bf16[1024,1024]{0,1:T(8,128)(2,1)} async-done(((bf16[128,1024]{0,1:T(8,128)(2,1)}), bf16[1024,1024]{0,1:T(8,128)(2,1)}) %all-gather.16.cloned.1.call-update) | async-done | bytes 2097168 | tf_op jit(solution)/shard_map/all_gather | solution.py:104
  187.4 3.9 copy.57
  191.3 60.5 %all-gather.18.cloned.1.call-done = bf16[1024,2048]{1,0:T(8,128)(2,1)} async-done(((bf16[32,2048]{1,0:T(8,128)(2,1)}), bf16[1024,2048]{1,0:T(8,128)(2,1)}) %all-gather.18.cloned.1.call-update) | async-done | bytes 4194320 | tf_op jit(solution)/shard_map/all_gather | solution.py:75
  251.9 6.4 copy.55
  258.3 3.5 multiply_reduce_fusion.3
  264.0 33.8 %while.36 = (s32[]{:T(128)}, bf16[128,8,2,128]{0,3,2,1:T(8,128)(2,1)S(1)}, f32[8,2,128]{2,1,0:T(2,128)}, bf16[1024,8,128]{0,2,1:T(8,128)(2,1)}, bf16[1024,8,128]...) while((s32[]{:T(128)}, ...), condition=%wide.region_6.7_spmd.clone.clone, body=%wide.region_3.6_spmd.clone.sunk.clone | while | flops 136445696 | bytes 4143713 | solution.py:148
  295.9 1.4 fusion.187
  297.8 17.3 %all-gather.20.cloned.1.call-done = bf16[2048,1024]{1,0:T(8,128)(2,1)} async-done(((bf16[64,1024]{1,0:T(8,128)(2,1)}), bf16[2048,1024]{1,0:T(8,128)(2,1)}) %all-gather.20.cloned.1.call-update) | async-done | bytes 4194320 | tf_op jit(solution)/shard_map/all_gather | solution.py:80
  315.1 3.0 multiply_reduce_fusion.8
  318.3 67.6 %all-gather.22.cloned.1.call-done = bf16[1024,3072]{1,0:T(8,128)(2,1)} async-done(((bf16[32,3072]{1,0:T(8,128)(2,1)}), bf16[1024,3072]{1,0:T(8,128)(2,1)}) %all-gather.22.cloned.1.call-update) | async-done | bytes 6291472 | tf_op jit(solution)/shard_map/all_gather | solution.py:153
  386.0 5.0 fusion.115
  390.9 65.6 %all-gather.24.cloned.1.call-done = bf16[1024,3072]{1,0:T(8,128)(2,1)} async-done(((bf16[32,3072]{1,0:T(8,128)(2,1)}), bf16[1024,3072]{1,0:T(8,128)(2,1)}) %all-gather.24.cloned.1.call-update) | async-done | bytes 6291472 | tf_op jit(solution)/shard_map/all_gather | solution.py:154
  456.6 4.9 fusion.116
  461.5 65.7 %all-gather.26.cloned.1.call-done = bf16[3072,1024]{1,0:T(8,128)(2,1)} async-done(((bf16[96,1024]{1,0:T(8,128)(2,1)}), bf16[3072,1024]{1,0:T(8,128)(2,1)}) %all-gather.26.cloned.1.call-update) | async-done | bytes 6291472 | tf_op jit(solution)/shard_map/all_gather | solution.py:155
  527.2 7.0 multiply_convert_fusion
  534.2 5.6 fusion.117
  539.8 2.9 multiply_reduce_fusion.4
  543.7 1.5 convolution_convert_fusion
  546.4 81.1 %while.37 = (s32[]{:T(128)}, f32[128,8,2,128]{0,3,2,1:T(8,128)}, bf16[1024,8,128]{0,2,1:T(8,128)(2,1)}, bf16[1024,8,128]{0,2,1:T(8,128)(2,1)}, bf16[1024,8,128]{...) while((s32[]{:T(128)}, f32[128,8,2,128]{0,3,2,1:T(8,128)}, ...), condition=%wide.region_11.12_spmd.clone.clone, body=%wide.region_9.11_spmd.clone.sunk.clone | while | flops 339347968 | bytes 14166661 | solution.py:254
  551.5 2.1 fusion.198
  553.5 2.0 fusion.199
  561.6 2.1 fusion.198
  563.7 2.0 fusion.199
  571.7 2.1 fusion.198
  573.8 2.0 fusion.199
  581.9 2.1 fusion.198
  584.0 2.0 fusion.199
  592.0 2.1 fusion.198
  594.1 2.0 fusion.199
  602.2 2.1 fusion.198
  604.2 2.0 fusion.199
  612.3 2.1 fusion.198
  614.4 2.0 fusion.199
  622.4 2.1 fusion.198
  624.5 2.0 fusion.199
  627.5 3.9 copy.69
  631.5 1.5 copy-done.23
  633.1 2.5 copy.71
  637.1 10.5 fusion.56
  647.6 23.6 %reduce-scatter.25.cloned.1.call-done = bf16[128,1024]{1,0:T(8,128)(2,1)} async-done(((bf16[1024,1024]{1,0:T(8,128)(2,1)}), bf16[128,1024]{1,0:T(8,128)(2,1)}) %reduce-scatter.25.cloned.1.call-update) | async-done | bytes 262160
  673.1 2.8 fusion.93
  676.0 39.7 %reduce-scatter.27.cloned.1.call-done = bf16[128,1024]{1,0:T(8,128)(2,1)} async-done(((bf16[1024,1024]{1,0:T(8,128)(2,1)}), bf16[128,1024]{1,0:T(8,128)(2,1)}) %reduce-scatter.27.cloned.1.call-update) | async-done | bytes 262160
  715.7 3.8 fusion.100
  722.2 4.6 fusion.95
  728.2 5.1 fusion.97
  734.6 7.5 fusion.85
  743.3 5.3 fusion.63
  751.3 1.7 fusion.78
  753.0 39.4 %all-reduce.8 = (f32[1024]{0:T(1024)S(1)}, f32[128]{0:T(128)S(1)}, f32[128]{0:T(128)S(1)}, f32[1024]{0:T(1024)S(1)}) all-reduce(f32[1024]{0:T(1024)S(1)} %get-tuple-element.423, f32[128]{0:T(128)S(1)} %get-tuple-element.417, f32[128]{0:T(128)S(1)} %get-tuple-element.419, ...), channel_id=4, replica_groups=mesh['seq'=4,'ctx'=8] {'seq','ctx'}, use_global_device_ids=true, to_apply=%region_18.19.clone | all-reduce | flops 2304 | bytes 18432
  795.7 169.3 %reduce-scatter.21.cloned.1.call-done = f32[32,6144]{1,0:T(8,128)} async-done(((f32[1024,6144]{1,0:T(8,128)}), f32[32,6144]{1,0:T(8,128)}) %reduce-scatter.21.cloned.1.call-update) | async-done | bytes 786448 | tf_op jit(solution)/shard_map/reduce_scatter | solution.py:196
  965.1 2.0 fusion.113
  967.1 143.4 %reduce-scatter.15.cloned.1.call-done = f32[32,1024]{1,0:T(8,128)} async-done(((f32[1024,1024]{1,0:T(8,128)}), f32[32,1024]{1,0:T(8,128)}) %reduce-scatter.15.cloned.1.call-update) | async-done | bytes 131088 | tf_op jit(solution)/shard_map/reduce_scatter | solution.py:299
  1110.5 141.7 %reduce-scatter.17.cloned.1.call-done = f32[32,1024]{1,0:T(8,128)} async-done(((f32[1024,1024]{1,0:T(8,128)}), f32[32,1024]{1,0:T(8,128)}) %reduce-scatter.17.cloned.1.call-update) | async-done | bytes 131088 | tf_op jit(solution)/shard_map/reduce_scatter | solution.py:300
  1252.2 148.8 %reduce-scatter.13.cloned.1.call-done = f32[32,2048]{1,0:T(8,128)} async-done(((f32[1024,2048]{1,0:T(8,128)}), f32[32,2048]{1,0:T(8,128)}) %reduce-scatter.13.cloned.1.call-update) | async-done | bytes 262160 | tf_op jit(solution)/shard_map/reduce_scatter | solution.py:298
  1400.9 148.6 %reduce-scatter.19.cloned.1.call-done = f32[64,1024]{1,0:T(8,128)} async-done(((f32[2048,1024]{1,0:T(8,128)}), f32[64,1024]{1,0:T(8,128)}) %reduce-scatter.19.cloned.1.call-update) | async-done | bytes 262160 | tf_op jit(solution)/shard_map/reduce_scatter | solution.py:211
  1549.5 157.2 %reduce-scatter.23.cloned.1.call-done = f32[96,1024]{1,0:T(8,128)} async-done(((f32[3072,1024]{1,0:T(8,128)}), f32[96,1024]{1,0:T(8,128)}) %reduce-scatter.23.cloned.1.call-update) | async-done | bytes 393232 | tf_op jit(solution)/shard_map/reduce_scatter | solution.py:176
  (260 shorter events, 114.9 us)
Async XLA Ops:
  7.2 65.7 %copy-start.29 = (s32[1,1024]{1,0:T(1,128)S(1)}, s32[1,1024]{1,0:T(1,128)}, u32[]{:S(2)}) copy-start(s32[1,1024]{1,0:T(1,128)} %param.19) | copy-start | bytes 12292
  7.2 62.7 %all-gather.10.cloned.1.call-start = ((), (), s32[]{:S(2)}) async-start(), calls=%async_computation.8 | async-start | bytes 2162688 | tf_op jit(solution)/shard_map/all_gather | solution.py:77
  7.9 119.9 %all-gather.14.cloned.1.call-start = ((), (), s32[]{:S(2)}) async-start(), calls=%async_computation.10 | async-start | bytes 2162688 | tf_op jit(solution)/shard_map/all_gather | solution.py:76
  8.7 148.3 %all-gather.12.cloned.1.call-start = ((), (), s32[]{:S(2)}) async-start(), calls=%async_computation.9 | async-start | bytes 2359296 | tf_op jit(solution)/shard_map/all_gather | solution.py:107
  55.4 202.8 %copy-start.33 = (f32[128]{0:T(128)}, f32[128]{0:T(128)S(1)}, u32[]{:S(2)}) copy-start(f32[128]{0:T(128)S(1)} %add_rsqrt_fusion.3) | copy-start | bytes 1540
  72.8 114.6 %all-gather.16.cloned.1.call-start = ((), (), s32[]{:S(2)}) async-start(), calls=%async_computation.11 | async-start | bytes 2359296 | tf_op jit(solution)/shard_map/all_gather | solution.py:104
  72.9 58.9 %copy-start.36 = (f32[128]{0:T(128)}, f32[128]{0:T(128)S(1)}, u32[]{:S(2)}) copy-start(f32[128]{0:T(128)S(1)} %convert_element_type.132) | copy-start | bytes 1540
  73.7 188.4 %copy-start.24 = (f32[128,128]{0,1:T(8,128)}, f32[128,128]{0,1:T(8,128)S(1)}, u32[]{:S(2)}) copy-start(f32[128,128]{0,1:T(8,128)S(1)} %get-tuple-element.490) | copy-start | bytes 196612
  127.8 2.9 copy-start.1
  131.6 0.8 copy-start.4
  131.6 1.6 copy-start.30
  133.2 118.6 %all-gather.18.cloned.1.call-start = ((), (), s32[]{:S(2)}) async-start(), calls=%async_computation.12 | async-start | bytes 4325376 | tf_op jit(solution)/shard_map/all_gather | solution.py:75
  133.8 181.3 %all-gather.20.cloned.1.call-start = ((), (), s32[]{:S(2)}) async-start(), calls=%async_computation.13 | async-start | bytes 4325376 | tf_op jit(solution)/shard_map/all_gather | solution.py:80
  134.4 251.5 %all-gather.22.cloned.1.call-start = ((), (), s32[]{:S(2)}) async-start(), calls=%async_computation.14 | async-start | bytes 6488064 | tf_op jit(solution)/shard_map/all_gather | solution.py:153
  135.2 321.4 %all-gather.24.cloned.1.call-start = ((), (), s32[]{:S(2)}) async-start(), calls=%async_computation.15 | async-start | bytes 6488064 | tf_op jit(solution)/shard_map/all_gather | solution.py:154
  135.9 391.2 %all-gather.26.cloned.1.call-start = ((), (), s32[]{:S(2)}) async-start(), calls=%async_computation.16 | async-start | bytes 6488064 | tf_op jit(solution)/shard_map/all_gather | solution.py:155
  136.6 534.6 %reduce-scatter.25.cloned.1.call-start = ((), (), s32[]{:S(2)}) async-start(), calls=%async_computation.23 | async-start | bytes 2359296
  136.8 125.0 %copy-start.38 = (f32[128]{0:T(128)}, f32[128]{0:T(128)S(1)}, u32[]{:S(2)}) copy-start(f32[128]{0:T(128)S(1)} %convert_element_type.135) | copy-start | bytes 1540
  157.0 3.4 copy-start.12
  262.1 0.7 copy-start.39
  297.8 20.3 %copy-start.15 = (bf16[128,8,2,128]{0,3,2,1:T(8,128)(2,1)}, bf16[128,8,2,128]{0,3,2,1:T(8,128)(2,1)S(1)}, u32[]{:S(2)}) copy-start(bf16[128,8,2,128]{0,3,2,1:T(8,128)(2,1)S(1)} %get-tuple-element.309) | copy-start | bytes 1572868
  315.1 3.1 copy-start.32
  318.2 224.6 %copy-start.6 = (f32[128,1024]{1,0:T(8,128)}, f32[128,1024]{1,0:T(8,128)S(1)}, u32[]{:S(2)}) copy-start(f32[128,1024]{1,0:T(8,128)S(1)} %get-tuple-element.496) | copy-start | bytes 1572868
  318.3 138.2 %copy-start.13 = (bf16[128,1024]{1,0:T(8,128)(2,1)}, bf16[128,1024]{1,0:T(8,128)(2,1)S(1)}, u32[]{:S(2)}) copy-start(bf16[128,1024]{1,0:T(8,128)(2,1)S(1)} %multiply_convert_fusion.5) | copy-start | bytes 786436
  390.9 136.2 %copy-start.26 = (bf16[1,128,1024]{2,1,0:T(8,128)(2,1)S(1)}, bf16[1,128,1024]{2,1,0:T(8,128)(2,1)}, u32[]{:S(2)}) copy-start(bf16[1,128,1024]{2,1,0:T(8,128)(2,1)} %param.31) | copy-start | bytes 786436
  534.2 5.6 copy-start.19
  534.2 5.6 copy-start.21
  534.2 5.6 copy-start
  539.8 3.9 copy-start.2
  542.9 0.8 copy-start.8
  631.5 1.6 copy-start.23
  631.5 84.2 %reduce-scatter.27.cloned.1.call-start = ((), (), s32[]{:S(2)}) async-start(), calls=%async_computation.24 | async-start | bytes 2359296
  635.6 0.9 copy-start.14
  635.6 1.2 copy-start.20
  635.6 1.5 copy-start.22
  635.6 329.4 %reduce-scatter.21.cloned.1.call-start = ((), (), s32[]{:S(2)}) async-start(), calls=%async_computation.21 | async-start | bytes 25952256 | tf_op jit(solution)/shard_map/reduce_scatter | solution.py:196
  647.5 24.9 %copy-start.25 = (f32[128,128]{0,1:T(8,128)S(1)}, f32[128,128]{0,1:T(8,128)}, u32[]{:S(2)}) copy-start(f32[128,128]{0,1:T(8,128)} %copy-done.24) | copy-start | bytes 196612
  647.6 25.0 %copy-start.5 = (f32[128,8,128]{0,2,1:T(8,128)S(1)}, f32[128,8,128]{0,2,1:T(8,128)}, u32[]{:S(2)}) copy-start(f32[128,8,128]{0,2,1:T(8,128)} %copy-done.4) | copy-start | bytes 1572868
  647.6 25.0 %copy-start.31 = (f32[128,8]{0,1:T(8,128)S(1)}, f32[128,8]{0,1:T(8,128)}, u32[]{:S(2)}) copy-start(f32[128,8]{0,1:T(8,128)} %copy-done.30) | copy-start | bytes 12292
  647.6 25.0 %copy-start.37 = (f32[128]{0:T(128)S(1)}, f32[128]{0:T(128)}, u32[]{:S(2)}) copy-start(f32[128]{0:T(128)} %copy-done.36) | copy-start | bytes 1540
  647.6 462.9 %reduce-scatter.15.cloned.1.call-start = ((), (), s32[]{:S(2)}) async-start(), calls=%async_computation.18 | async-start | bytes 4325376 | tf_op jit(solution)/shard_map/reduce_scatter | solution.py:299
  672.5 0.7 copy-start.34
  676.0 576.2 %reduce-scatter.17.cloned.1.call-start = ((), (), s32[]{:S(2)}) async-start(), calls=%async_computation.19 | async-start | bytes 4325376 | tf_op jit(solution)/shard_map/reduce_scatter | solution.py:300
  719.5 1.2 copy-start.17
  719.5 681.4 %reduce-scatter.13.cloned.1.call-start = ((), (), s32[]{:S(2)}) async-start(), calls=%async_computation.17 | async-start | bytes 8650752 | tf_op jit(solution)/shard_map/reduce_scatter | solution.py:298
  720.7 0.7 copy-start.40
  726.7 1.2 copy-start.9
  726.8 1.5 copy-start.16
  726.8 822.7 %reduce-scatter.19.cloned.1.call-start = ((), (), s32[]{:S(2)}) async-start(), calls=%async_computation.20 | async-start | bytes 8650752 | tf_op jit(solution)/shard_map/reduce_scatter | solution.py:211
  733.3 1.2 copy-start.18
  733.3 1.3 copy-start.27
  733.3 973.4 %reduce-scatter.23.cloned.1.call-start = ((), (), s32[]{:S(2)}) async-start(), calls=%async_computation.22 | async-start | bytes 12976128 | tf_op jit(solution)/shard_map/reduce_scatter | solution.py:176
  742.2 1.1 copy-start.7
  743.3 5.3 copy-start.10
  743.3 5.3 copy-start.28
  743.3 6.2 copy-start.11
  748.6 2.7 copy-start.3
  751.3 1.7 copy-start.35
Sparse Core Ops, SparseCore 0:
  10.9 58.9 all-gather.9
  72.7 55.0 all-gather.13
  130.3 26.6 all-gather.11
  159.3 28.0 all-gather.15
  190.1 61.7 all-gather.17
  254.6 60.5 all-gather.19
  318.0 67.9 all-gather.21
  388.8 67.6 all-gather.23
  459.4 67.6 all-gather.25
  631.6 39.6 reduce-scatter.24
  674.6 41.0 reduce-scatter.26
  722.0 243.0 reduce-scatter.20
  967.9 142.5 reduce-scatter.14
  1113.2 138.9 reduce-scatter.16
  1254.9 145.9 reduce-scatter.12
  1403.7 145.8 reduce-scatter.18
  1556.0 150.7 reduce-scatter.22
where the time goes:
time: 1720 us; the launch traced here: 1710 us
  waiting for transfers between devices  1370 us (80%)
  matrix products  163 us (9%)
  blocking collectives  81.5 us (5%)
  local copies, waits for them, and re-layouts  61.5 us (4%)
  other arithmetic  26.8 us (2%)
    reduce_scatter x1, waiting for transfers between devices, local(): lax.psum_scatter(jnp.dot(second_input.T, both_low, preferred_element_type...  169 us
    reduce_scatter x1, waiting for transfers between devices, local(): lax.psum_scatter(jnp.dot(activation.T, upstream_low, preferred_element_ty...  157 us
    reduce_scatter x1, waiting for transfers between devices, local(): lax.psum_scatter(query_term, ('seq', 'ctx'), scatter_dimension=0, tiled=T...  149 us
    reduce_scatter x1, waiting for transfers between devices, local(): lax.psum_scatter(jnp.dot(attention_low.T, middle_low, preferred_element_t...  149 us
    reduce_scatter x1, waiting for transfers between devices, local(): lax.psum_scatter(key_term, ('seq', 'ctx'), scatter_dimension=0, tiled=True)  143 us
    reduce_scatter x1, waiting for transfers between devices, local(): lax.psum_scatter(value_term, ('seq', 'ctx'), scatter_dimension=0, tiled=T...  142 us
    unnamed x2, blocking collectives  81.5 us
    unnamed x19, waiting for transfers between devices  68 us
  transfers between devices with their start and end apart: 17, of which 17 were waited for; matrix products, arithmetic and copies ran while one was open for 8% of the time, Pallas kernels for 0%

commit v1 on v0

--- a/solution.py
+++ b/solution.py
@@ -150,7 +150,15 @@
     middle = residual + jnp.dot(attention_low, output_full, preferred_element_type=jnp.float32)
     second_gains, gate_full, up_full, down_full = (
         lax.all_gather(gain_second, ("seq", "ctx"), axis=0, tiled=True),
-        lax.all_gather(weight_gate, ("seq", "ctx"), axis=0, tiled=True),
+        jnp.concatenate(
+            lax.all_to_all(
+                jnp.stack([weight_gate for _ in range(lax.psum(1, ("seq", "ctx")))], axis=0),
+                ("seq", "ctx"),
+                0,
+                0,
+            ),
+            axis=0,
+        ),
         lax.all_gather(weight_up, ("seq", "ctx"), axis=0, tiled=True),
         lax.all_gather(weight_down, ("seq", "ctx"), axis=0, tiled=True),
     )

time: 1720 us -> 1770 us (1.029)
  waiting for transfers between devices: 1370 us -> 1410 us
    all_gather x1, waiting for transfers between devices: 23.4 us -> 48.6 us  [local(): lax.all_gather(key_rotated.reshape(tokens, key_head_rows * head_size), 'c...]
    unnamed x102 -> x104, local copies, waits for them, and re-layouts: 36.4 us -> 36.4 us
  transfers between devices with their start and end apart: 17 -> 18, of which waited for: 17 -> 17; matrix products, arithmetic and copies ran while one was open for 8% -> 8% of each run, Pallas kernels for 0% -> 0%
where the time goes in v1:
time: 1770 us
  waiting for transfers between devices  1410 us (80%)
  matrix products  162 us (9%)
  blocking collectives  81.6 us (5%)
  local copies, waits for them, and re-layouts  65 us (4%)
  other arithmetic  26.8 us (2%)
    reduce_scatter x1, waiting for transfers between devices, local(): lax.psum_scatter(jnp.dot(second_input.T, both_low, preferred_element_type...  169 us
    reduce_scatter x1, waiting for transfers between devices, local(): lax.psum_scatter(jnp.dot(activation.T, upstream_low, preferred_element_ty...  157 us
    reduce_scatter x1, waiting for transfers between devices, local(): lax.psum_scatter(query_term, ('seq', 'ctx'), scatter_dimension=0, tiled=T...  149 us
    reduce_scatter x1, waiting for transfers between devices, local(): lax.psum_scatter(jnp.dot(attention_low.T, middle_low, preferred_element_t...  149 us
    reduce_scatter x1, waiting for transfers between devices, local(): lax.psum_scatter(key_term, ('seq', 'ctx'), scatter_dimension=0, tiled=True)  143 us
    reduce_scatter x1, waiting for transfers between devices, local(): lax.psum_scatter(value_term, ('seq', 'ctx'), scatter_dimension=0, tiled=T...  142 us
    unnamed x2, blocking collectives  81.6 us
    all_gather x1, waiting for transfers between devices, local(): lax.all_gather(weight_query, ('seq', 'ctx'), axis=0, tiled=True)  72.3 us
  transfers between devices with their start and end apart: 18, of which 17 were waited for; matrix products, arithmetic and copies ran while one was open for 8% of the time, Pallas kernels for 0%

profile of v1, /device:TPU:0, one launch (start us, length us, event | category | flops | bytes accessed | tf_op | source)
XLA Modules:
  0.0 1767.1 jit_solution(12413437650613683897)
XLA Ops:
  12.1 42.2 %all-reduce.9 = (bf16[1024]{0:T(1024)(128)(2,1)S(1)}, bf16[128]{0:T(256)(128)(2,1)S(1)}, bf16[128]{0:T(256)(128)(2,1)S(1)}, bf16[1024]{0:T(1024)(128)(2,1)S(1)}) all-reduce(bf16[1024]{0:T(1024)(128)(2,1)S(1)} %dynamic-update-slice, bf16[128]{0:T(256)(128)(2,1)S(1)} %dynamic-update-slice.1, ...), channel_id=1, replica_groups=mesh['seq'=4,'ctx'=8] {'seq','ctx'}, use_global_device_ids=true, to_apply=%add | all-reduce | flops 2304 | bytes 9216
  55.5 14.4 all-gather.10.cloned.1.call-done
  69.9 2.9 convolution_convert_fusion.1
  73.8 54.1 %all-gather.14.cloned.1.call-done = bf16[1024,1024]{1,0:T(8,128)(2,1)} async-done(((bf16[32,1024]{1,0:T(8,128)(2,1)}), bf16[1024,1024]{1,0:T(8,128)(2,1)}) %all-gather.14.cloned.1.call-update) | async-done | bytes 2097168 | tf_op jit(solution)/shard_map/all_gather | solution.py:76
  127.8 2.9 copy.54
  135.9 3.4 stack.2
  139.4 3.6 all-to-all-start
  144.5 36.6 %all-gather.12.cloned.1.call-done = bf16[1024,1024]{1,0:T(8,128)(2,1)} async-done(((bf16[128,1024]{1,0:T(8,128)(2,1)}), bf16[1024,1024]{1,0:T(8,128)(2,1)}) %all-gather.12.cloned.1.call-update) | async-done | bytes 2097168 | tf_op jit(solution)/shard_map/all_gather | solution.py:107
  181.2 2.2 copy.91
  183.4 3.0 copy.56
  186.4 48.6 %all-gather.16.cloned.1.call-done = bf16[1024,1024]{0,1:T(8,128)(2,1)} async-done(((bf16[128,1024]{0,1:T(8,128)(2,1)}), bf16[1024,1024]{0,1:T(8,128)(2,1)}) %all-gather.16.cloned.1.call-update) | async-done | bytes 2097168 | tf_op jit(solution)/shard_map/all_gather | solution.py:104
  235.0 4.1 copy.57
  239.0 1.8 copy_bitcast_fusion.3
  240.8 72.3 %all-gather.18.cloned.1.call-done = bf16[1024,2048]{1,0:T(8,128)(2,1)} async-done(((bf16[32,2048]{1,0:T(8,128)(2,1)}), bf16[1024,2048]{1,0:T(8,128)(2,1)}) %all-gather.18.cloned.1.call-update) | async-done | bytes 4194320 | tf_op jit(solution)/shard_map/all_gather | solution.py:75
  313.1 6.4 copy.55
  319.5 3.5 multiply_reduce_fusion.3
  325.3 33.8 %while.36 = (s32[]{:T(128)}, bf16[128,8,2,128]{0,3,2,1:T(8,128)(2,1)S(1)}, f32[8,2,128]{2,1,0:T(2,128)}, bf16[1024,8,128]{0,2,1:T(8,128)(2,1)}, bf16[1024,8,128]...) while((s32[]{:T(128)}, ...), condition=%wide.region_6.7_spmd.clone.clone, body=%wide.region_3.6_spmd.clone.sunk.clone | while | flops 136445696 | bytes 4143713 | solution.py:148
  359.1 17.3 all-gather.20.cloned.1.call-done
  376.4 3.0 multiply_reduce_fusion.8
  379.6 5.0 fusion.115
  384.6 62.6 %all-gather.22.cloned.1.call-done = bf16[1024,3072]{1,0:T(8,128)(2,1)} async-done(((bf16[32,3072]{1,0:T(8,128)(2,1)}), bf16[1024,3072]{1,0:T(8,128)(2,1)}) %all-gather.22.cloned.1.call-update) | async-done | bytes 6291472 | tf_op jit(solution)/shard_map/all_gather | solution.py:162
  447.2 5.0 fusion.116
  452.2 65.6 %all-gather.24.cloned.1.call-done = bf16[3072,1024]{1,0:T(8,128)(2,1)} async-done(((bf16[96,1024]{1,0:T(8,128)(2,1)}), bf16[3072,1024]{1,0:T(8,128)(2,1)}) %all-gather.24.cloned.1.call-update) | async-done | bytes 6291472 | tf_op jit(solution)/shard_map/all_gather | solution.py:163
  517.8 7.1 multiply_convert_fusion
  524.9 63.5 %all-gather.26.cloned.1.call-done = bf16[1024,3072]{1,0:T(8,128)(2,1)} async-done(((bf16[32,3072]{1,0:T(8,128)(2,1)}), bf16[1024,3072]{1,0:T(8,128)(2,1)}) %all-gather.26.cloned.1.call-update) | async-done | bytes 6291472 | tf_op jit(solution)/shard_map/all_gather | solution.py:178
  588.4 5.1 fusion.117
  593.6 2.9 multiply_reduce_fusion.4
  600.3 81.0 %while.37 = (s32[]{:T(128)}, f32[128,8,2,128]{0,3,2,1:T(8,128)}, bf16[1024,8,128]{0,2,1:T(8,128)(2,1)}, bf16[1024,8,128]{0,2,1:T(8,128)(2,1)}, bf16[1024,8,128]{...) while((s32[]{:T(128)}, f32[128,8,2,128]{0,3,2,1:T(8,128)}, ...), condition=%wide.region_11.12_spmd.clone.clone, body=%wide.region_9.11_spmd.clone.sunk.clone | while | flops 339347968 | bytes 14166661 | solution.py:262
  605.3 2.1 fusion.198
  607.4 2.0 fusion.199
  615.4 2.1 fusion.198
  617.5 2.0 fusion.199
  625.6 2.1 fusion.198
  627.6 2.0 fusion.199
  635.7 2.1 fusion.198
  637.7 2.0 fusion.199
  645.8 2.1 fusion.198
  647.9 2.0 fusion.199
  655.9 2.1 fusion.198
  658.0 2.0 fusion.199
  666.0 2.1 fusion.198
  668.1 2.0 fusion.199
  676.2 2.1 fusion.198
  678.2 2.0 fusion.199
  681.3 3.9 copy.69
  686.8 2.5 copy.71
  690.8 10.4 fusion.56
  701.4 23.7 %reduce-scatter.25.cloned.1.call-done = bf16[128,1024]{1,0:T(8,128)(2,1)} async-done(((bf16[1024,1024]{1,0:T(8,128)(2,1)}), bf16[128,1024]{1,0:T(8,128)(2,1)}) %reduce-scatter.25.cloned.1.call-update) | async-done | bytes 262160
  726.9 2.8 fusion.93
  729.8 39.7 %reduce-scatter.27.cloned.1.call-done = bf16[128,1024]{1,0:T(8,128)(2,1)} async-done(((bf16[1024,1024]{1,0:T(8,128)(2,1)}), bf16[128,1024]{1,0:T(8,128)(2,1)}) %reduce-scatter.27.cloned.1.call-update) | async-done | bytes 262160
  769.5 3.8 fusion.100
  775.9 4.6 fusion.95
  781.9 5.1 fusion.97
  788.4 7.5 fusion.85
  797.0 5.3 fusion.63
  805.1 1.7 fusion.78
  806.8 39.4 %all-reduce.8 = (f32[1024]{0:T(1024)S(1)}, f32[128]{0:T(128)S(1)}, f32[128]{0:T(128)S(1)}, f32[1024]{0:T(1024)S(1)}) all-reduce(f32[1024]{0:T(1024)S(1)} %get-tuple-element.423, f32[128]{0:T(128)S(1)} %get-tuple-element.417, f32[128]{0:T(128)S(1)} %get-tuple-element.419, ...), channel_id=4, replica_groups=mesh['seq'=4,'ctx'=8] {'seq','ctx'}, use_global_device_ids=true, to_apply=%region_18.19.clone | all-reduce | flops 2304 | bytes 18432
  849.5 169.3 %reduce-scatter.21.cloned.1.call-done = f32[32,6144]{1,0:T(8,128)} async-done(((f32[1024,6144]{1,0:T(8,128)}), f32[32,6144]{1,0:T(8,128)}) %reduce-scatter.21.cloned.1.call-update) | async-done | bytes 786448 | tf_op jit(solution)/shard_map/reduce_scatter | solution.py:204
  1018.8 2.0 fusion.113
  1020.9 143.4 %reduce-scatter.15.cloned.1.call-done = f32[32,1024]{1,0:T(8,128)} async-done(((f32[1024,1024]{1,0:T(8,128)}), f32[32,1024]{1,0:T(8,128)}) %reduce-scatter.15.cloned.1.call-update) | async-done | bytes 131088 | tf_op jit(solution)/shard_map/reduce_scatter | solution.py:307
  1164.2 141.6 %reduce-scatter.17.cloned.1.call-done = f32[32,1024]{1,0:T(8,128)} async-done(((f32[1024,1024]{1,0:T(8,128)}), f32[32,1024]{1,0:T(8,128)}) %reduce-scatter.17.cloned.1.call-update) | async-done | bytes 131088 | tf_op jit(solution)/shard_map/reduce_scatter | solution.py:308
  1305.9 149.0 %reduce-scatter.13.cloned.1.call-done = f32[32,2048]{1,0:T(8,128)} async-done(((f32[1024,2048]{1,0:T(8,128)}), f32[32,2048]{1,0:T(8,128)}) %reduce-scatter.13.cloned.1.call-update) | async-done | bytes 262160 | tf_op jit(solution)/shard_map/reduce_scatter | solution.py:306
  1454.8 148.6 %reduce-scatter.19.cloned.1.call-done = f32[64,1024]{1,0:T(8,128)} async-done(((f32[2048,1024]{1,0:T(8,128)}), f32[64,1024]{1,0:T(8,128)}) %reduce-scatter.19.cloned.1.call-update) | async-done | bytes 262160 | tf_op jit(solution)/shard_map/reduce_scatter | solution.py:219
  1603.4 157.1 %reduce-scatter.23.cloned.1.call-done = f32[96,1024]{1,0:T(8,128)} async-done(((f32[3072,1024]{1,0:T(8,128)}), f32[96,1024]{1,0:T(8,128)}) %reduce-scatter.23.cloned.1.call-update) | async-done | bytes 393232 | tf_op jit(solution)/shard_map/reduce_scatter | solution.py:184
  (265 shorter events, 118.7 us)
Async XLA Ops:
  7.2 65.7 %copy-start.30 = (s32[1,1024]{1,0:T(1,128)S(1)}, s32[1,1024]{1,0:T(1,128)}, u32[]{:S(2)}) copy-start(s32[1,1024]{1,0:T(1,128)} %param.19) | copy-start | bytes 12292
  7.2 62.7 %all-gather.10.cloned.1.call-start = ((), (), s32[]{:S(2)}) async-start(), calls=%async_computation.9 | async-start | bytes 2162688 | tf_op jit(solution)/shard_map/all_gather | solution.py:77
  7.9 119.9 %all-gather.14.cloned.1.call-start = ((), (), s32[]{:S(2)}) async-start(), calls=%async_computation.11 | async-start | bytes 2162688 | tf_op jit(solution)/shard_map/all_gather | solution.py:76
  8.7 172.5 %all-gather.12.cloned.1.call-start = ((), (), s32[]{:S(2)}) async-start(), calls=%async_computation.10 | async-start | bytes 2359296 | tf_op jit(solution)/shard_map/all_gather | solution.py:107
  55.5 264.1 %copy-start.34 = (f32[128]{0:T(128)}, f32[128]{0:T(128)S(1)}, u32[]{:S(2)}) copy-start(f32[128]{0:T(128)S(1)} %add_rsqrt_fusion.3) | copy-start | bytes 1540
  72.8 162.1 %all-gather.16.cloned.1.call-start = ((), (), s32[]{:S(2)}) async-start(), calls=%async_computation.12 | async-start | bytes 2359296 | tf_op jit(solution)/shard_map/all_gather | solution.py:104
  72.9 58.9 %copy-start.37 = (f32[128]{0:T(128)}, f32[128]{0:T(128)S(1)}, u32[]{:S(2)}) copy-start(f32[128]{0:T(128)S(1)} %convert_element_type.132) | copy-start | bytes 1540
  73.7 249.7 %copy-start.24 = (f32[128,128]{0,1:T(8,128)}, f32[128,128]{0,1:T(8,128)S(1)}, u32[]{:S(2)}) copy-start(f32[128,128]{0,1:T(8,128)S(1)} %get-tuple-element.490) | copy-start | bytes 196612
  127.8 2.9 copy-start.1
  131.6 0.8 copy-start.4
  131.6 3.6 copy-start.31
  131.6 4.3 copy-start.29
  133.2 179.9 %all-gather.18.cloned.1.call-start = ((), (), s32[]{:S(2)}) async-start(), calls=%async_computation.13 | async-start | bytes 4325376 | tf_op jit(solution)/shard_map/all_gather | solution.py:75
  133.8 242.5 %all-gather.20.cloned.1.call-start = ((), (), s32[]{:S(2)}) async-start(), calls=%async_computation.14 | async-start | bytes 4325376 | tf_op jit(solution)/shard_map/all_gather | solution.py:80
  134.4 312.8 %all-gather.22.cloned.1.call-start = ((), (), s32[]{:S(2)}) async-start(), calls=%async_computation.15 | async-start | bytes 6488064 | tf_op jit(solution)/shard_map/all_gather | solution.py:162
  135.2 382.6 %all-gather.24.cloned.1.call-start = ((), (), s32[]{:S(2)}) async-start(), calls=%async_computation.16 | async-start | bytes 6488064 | tf_op jit(solution)/shard_map/all_gather | solution.py:163
  139.4 240.2 %all-to-all-start = ((bf16[32,32,3072]{2,1,0:T(8,128)(2,1)}), bf16[32,32,3072]{2,1,0:T(8,128)(2,1)}, u32[]{:S(2)}, u32[]{:S(2)}) async-start(bf16[32,32,3072]{2,1,0:T(8,128)(2,1)} %stack.2), calls=%async_computation | async-start | bytes 12582912 | tf_op jit(solution)/shard_map/all_to_all | solution.py:154
  143.0 445.4 %all-gather.26.cloned.1.call-start = ((), (), s32[]{:S(2)}) async-start(), calls=%async_computation.17 | async-start | bytes 6488064 | tf_op jit(solution)/shard_map/all_gather | solution.py:178
  143.7 581.3 %reduce-scatter.25.cloned.1.call-start = ((), (), s32[]{:S(2)}) async-start(), calls=%async_computation.24 | async-start | bytes 2359296
  143.8 179.3 %copy-start.39 = (f32[128]{0:T(128)}, f32[128]{0:T(128)S(1)}, u32[]{:S(2)}) copy-start(f32[128]{0:T(128)S(1)} %convert_element_type.135) | copy-start | bytes 1540
  235.0 4.1 copy-start.12
  323.3 0.7 copy-start.40
  359.1 20.3 %copy-start.15 = (bf16[128,8,2,128]{0,3,2,1:T(8,128)(2,1)}, bf16[128,8,2,128]{0,3,2,1:T(8,128)(2,1)S(1)}, u32[]{:S(2)}) copy-start(bf16[128,8,2,128]{0,3,2,1:T(8,128)(2,1)S(1)} %get-tuple-element.309) | copy-start | bytes 1572868
  376.4 3.1 copy-start.33
  379.4 217.1 %copy-start.6 = (f32[128,1024]{1,0:T(8,128)}, f32[128,1024]{1,0:T(8,128)S(1)}, u32[]{:S(2)}) copy-start(f32[128,1024]{1,0:T(8,128)S(1)} %get-tuple-element.496) | copy-start | bytes 1572868
  379.5 67.7 %copy-start.13 = (bf16[128,1024]{1,0:T(8,128)(2,1)}, bf16[128,1024]{1,0:T(8,128)(2,1)S(1)}, u32[]{:S(2)}) copy-start(bf16[128,1024]{1,0:T(8,128)(2,1)S(1)} %multiply_convert_fusion.5) | copy-start | bytes 786436
  524.9 68.6 %copy-start.19 = (bf16[128,3072]{1,0:T(8,128)(2,1)}, bf16[128,3072]{1,0:T(8,128)(2,1)S(1)}, u32[]{:S(2)}) copy-start(bf16[128,3072]{1,0:T(8,128)(2,1)S(1)} %get-tuple-element.477) | copy-start | bytes 2359300
  524.9 68.6 %copy-start.21 = (bf16[128,3072]{1,0:T(8,128)(2,1)}, bf16[128,3072]{1,0:T(8,128)(2,1)S(1)}, u32[]{:S(2)}) copy-start(bf16[128,3072]{1,0:T(8,128)(2,1)S(1)} %get-tuple-element.476) | copy-start | bytes 2359300
  588.4 5.2 copy-start
  593.6 3.0 copy-start.26
  593.6 4.0 copy-start.2
  596.7 0.8 copy-start.8
  685.2 1.6 copy-start.23
  685.2 84.2 %reduce-scatter.27.cloned.1.call-start = ((), (), s32[]{:S(2)}) async-start(), calls=%async_computation.25 | async-start | bytes 2359296
  689.3 0.9 copy-start.14
  689.3 1.2 copy-start.20
  689.3 1.5 copy-start.22
  689.4 329.5 %reduce-scatter.21.cloned.1.call-start = ((), (), s32[]{:S(2)}) async-start(), calls=%async_computation.22 | async-start | bytes 25952256 | tf_op jit(solution)/shard_map/reduce_scatter | solution.py:204
  701.2 24.9 %copy-start.25 = (f32[128,128]{0,1:T(8,128)S(1)}, f32[128,128]{0,1:T(8,128)}, u32[]{:S(2)}) copy-start(f32[128,128]{0,1:T(8,128)} %copy-done.24) | copy-start | bytes 196612
  701.3 25.0 %copy-start.5 = (f32[128,8,128]{0,2,1:T(8,128)S(1)}, f32[128,8,128]{0,2,1:T(8,128)}, u32[]{:S(2)}) copy-start(f32[128,8,128]{0,2,1:T(8,128)} %copy-done.4) | copy-start | bytes 1572868
  701.3 25.0 %copy-start.32 = (f32[128,8]{0,1:T(8,128)S(1)}, f32[128,8]{0,1:T(8,128)}, u32[]{:S(2)}) copy-start(f32[128,8]{0,1:T(8,128)} %copy-done.31) | copy-start | bytes 12292
  701.3 25.0 %copy-start.38 = (f32[128]{0:T(128)S(1)}, f32[128]{0:T(128)}, u32[]{:S(2)}) copy-start(f32[128]{0:T(128)} %copy-done.37) | copy-start | bytes 1540
  701.3 462.9 %reduce-scatter.15.cloned.1.call-start = ((), (), s32[]{:S(2)}) async-start(), calls=%async_computation.19 | async-start | bytes 4325376 | tf_op jit(solution)/shard_map/reduce_scatter | solution.py:307
  726.2 0.7 copy-start.35
  729.7 576.1 %reduce-scatter.17.cloned.1.call-start = ((), (), s32[]{:S(2)}) async-start(), calls=%async_computation.20 | async-start | bytes 4325376 | tf_op jit(solution)/shard_map/reduce_scatter | solution.py:308
  773.2 1.2 copy-start.17
  773.3 681.6 %reduce-scatter.13.cloned.1.call-start = ((), (), s32[]{:S(2)}) async-start(), calls=%async_computation.18 | async-start | bytes 8650752 | tf_op jit(solution)/shard_map/reduce_scatter | solution.py:306
  774.5 0.7 copy-start.41
  780.5 1.2 copy-start.9
  780.5 1.4 copy-start.16
  780.5 822.9 %reduce-scatter.19.cloned.1.call-start = ((), (), s32[]{:S(2)}) async-start(), calls=%async_computation.21 | async-start | bytes 8650752 | tf_op jit(solution)/shard_map/reduce_scatter | solution.py:219
  787.1 1.2 copy-start.18
  787.1 1.3 copy-start.27
  787.1 973.5 %reduce-scatter.23.cloned.1.call-start = ((), (), s32[]{:S(2)}) async-start(), calls=%async_computation.23 | async-start | bytes 12976128 | tf_op jit(solution)/shard_map/reduce_scatter | solution.py:184
  795.9 1.1 copy-start.7
  797.0 5.3 copy-start.10
  797.0 5.3 copy-start.28
  797.0 6.2 copy-start.11
  802.3 2.7 copy-start.3
  805.1 1.7 copy-start.36
Sparse Core Ops, SparseCore 0:
  10.9 58.9 all-gather.9
  72.7 55.0 all-gather.13
  130.3 50.8 all-gather.11
  183.5 51.4 all-gather.15
  237.7 75.3 all-gather.17
  315.8 60.5 all-gather.19
  379.2 67.9 all-gather.21
  450.1 67.6 all-gather.23
  520.7 67.6 all-gather.25
  685.4 39.6 reduce-scatter.24
  728.3 41.0 reduce-scatter.26
  775.7 243.0 reduce-scatter.20
  1021.7 142.5 reduce-scatter.14
  1166.9 138.8 reduce-scatter.16
  1308.6 146.1 reduce-scatter.12
  1457.5 145.8 reduce-scatter.18
  1609.9 150.6 reduce-scatter.22
